TPU v7x, 128 devices: a whole 4x4x4 slice. The times are simulated.
128 devices in a mesh: row: 8 (over z_hi, x), col: 16 (over z_lo, y, core).
Axes of the slice: x: 4, y: 4, z: 4 (z_hi: 2, z_lo: 2; z = z_hi * 2 + z_lo), core: 2. Of those that a mesh axis runs over, the one named last changes fastest.
Arguments:
- diag_blocks: float32 [2, 512, 512], replicated, may hold values from -1 to 5, as said below
- pivot_flags: int32 [2, 512], replicated, may hold values 0 or 1
- panels: bfloat16 [2, 32768, 512], P(None, ('row', 'col')), may hold values from -3 to 3
- structure: int32 [2, 32768], P(None, ('row', 'col')), may hold values 0 or 1
- ancestor_inverse: bfloat16 [32768, 32768], P('row', 'col'), may hold values from -0.046875 to 0.046875
Outputs:
- inverse_panel: bfloat16 [2, 32768, 512], P(None, ('row', 'col'))
- inverse_diagonal: float32 [2, 512, 512], replicated
Inputs may be any that keep to these rules, and one draw needn't show every extreme that they name: Each diag_blocks[k] is symmetric, and its off-diagonal part is small enough that every eigenvalue of each shifted block is at least 0.8, so every shifted block is positive definite.
All inputs are finite; a program needn't handle non-finite values. No bound on the sum of `structure` on one device may be relied on, other than what follows from the above.
Results may differ from a plain program's by a relative error of at most 0.0051.
Values may be sent and summed in bfloat16 or wider, within the bound.
No kernel may reach another device: no remote copies, remote signals or barrier semaphores. Data moves between devices by JAX's collectives and lax.ppermute only.
A program may use at most 192 MiB of HBM per device.

v0:
```python
import jax
import jax.numpy as jnp
from jax import lax
from jax.sharding import PartitionSpec as P

HIGHEST_PRECISION = lax.Precision.HIGHEST
PERTURBATION = 1.0


def from_root(value, axis, source):
    kept = jnp.where(lax.axis_index(axis) == source, value, 0).astype(value.dtype)
    return lax.psum(kept, axis)


def factor_inverse(diagonal_block, flag_row):
    node_width = diagonal_block.shape[0]
    identity = jnp.eye(node_width, dtype=jnp.float32)
    shifted = diagonal_block + PERTURBATION * identity * flag_row.astype(jnp.float32)[None, :]
    factor_lower = jnp.linalg.cholesky(shifted)
    lower_inverse = jax.scipy.linalg.solve_triangular(factor_lower, identity, lower=True)
    return jnp.dot(lower_inverse.T, lower_inverse, precision=HIGHEST_PRECISION)


def normalize_panel(panel_rows, member_row, inverse):
    masked = panel_rows.astype(jnp.float32) * member_row.astype(jnp.float32)[:, None]
    return jnp.dot(masked, inverse, precision=HIGHEST_PRECISION).astype(jnp.bfloat16)


def exact_contract(left_rows, right_rows):
    dims = (((0,), (0,)), ((), ()))
    return lax.dot_general(
        left_rows.astype(jnp.float32),
        right_rows,
        dims,
        precision=HIGHEST_PRECISION,
        preferred_element_type=jnp.float32,
    )


def local(diag_blocks, pivot_flags, panels, structure, ancestor_inverse):
    node_count = diag_blocks.shape[0]
    node_width = diag_blocks.shape[2]
    inverses = [
        factor_inverse(diag_blocks[supernode], pivot_flags[supernode])
        for supernode in range(node_count)
    ]
    normed = [
        normalize_panel(panels[supernode], structure[supernode], inverses[supernode])
        for supernode in range(node_count)
    ]
    groups = jnp.concatenate(normed, axis=1)
    col_ratio = lax.axis_size("col") // lax.axis_size("row")
    col_index = lax.axis_index("col")
    own_rows = ancestor_inverse.shape[0] // lax.axis_size("col")
    panel_terms = []
    diagonal_terms = []
    row_block = lax.all_gather(groups, "col", axis=0, tiled=True)
    block_rows = row_block.shape[0] // col_ratio
    column_part = lax.dynamic_slice_in_dim(
        row_block, col_index % col_ratio * block_rows, block_rows, 0
    )
    column_block = from_root(column_part, "row", col_index // col_ratio)
    group_size = groups.shape[1] // node_width

    def product(offset, row_count, column_block=column_block):
        return jnp.dot(ancestor_inverse, column_block, preferred_element_type=jnp.float32)

    summed = lax.psum_scatter(
        product(jnp.int32(0), own_rows * lax.axis_size("col")),
        "col",
        scatter_dimension=0,
        tiled=True,
    )
    for member in range(group_size):
        lower_col = member * node_width
        diagonal_terms.append(
            exact_contract(
                groups[:, lower_col : lower_col + node_width],
                summed[:, lower_col : lower_col + node_width],
            )
        )
    for member in range(group_size):
        lower_col = member * node_width
        panel_terms.append(summed[:, lower_col : lower_col + node_width])
    totals = lax.psum(jnp.stack(diagonal_terms), ("row", "col"))
    inverse_diagonal = jnp.stack(inverses) + totals
    inverse_panel = (-jnp.stack(panel_terms)).astype(jnp.bfloat16)
    return (inverse_panel, inverse_diagonal)


def solution(mesh):
    in_specs = (P(), P(), P(None, ("row", "col"), None), P(None, ("row", "col")), P("row", "col"))
    out_specs = (P(None, ("row", "col"), None), P())
    return jax.shard_map(local, mesh=mesh, in_specs=in_specs, out_specs=out_specs, check_vma=False)
```

profile of v0, /device:TPU:1, one launch (start us, length us, event | category | flops | bytes accessed | tf_op | source)
XLA Modules:
  0.0 775.6 jit_solution(5468474773533071747)
XLA Ops:
  8.9 2.7 fusion.90
  11.9 1.6 copy.13
  14.6 2.5 copy.10
  17.1 1.5 fusion.17
  19.6 11.7 %cholesky.358 = f32[128,128]{1,0:T(8,128)S(1)} custom-call(f32[128,128]{1,0:T(8,128)S(1)} %cholesky.439), custom_call_target="Cholesky" | custom-call | tf_op jit(solution)/shard_map/jit(cholesky)/cholesky | solution.py:19
  31.3 9.8 %custom-call.31 = f32[1,128,128]{1,2,0:T(8,128)S(1)} custom-call(f32[1,128,128]{2,1,0:T(8,128)S(1)} %get-tuple-element.65), custom_call_target="InvertDiagBlocksLowerTriangular" | custom-call | tf_op jit(solution)/shard_map/jit(cholesky)/cholesky | solution.py:19
  43.8 11.7 %cholesky.377 = f32[128,128]{1,0:T(8,128)S(1)} custom-call(f32[128,128]{1,0:T(8,128)S(1)} %cholesky.443), custom_call_target="Cholesky" | custom-call | tf_op jit(solution)/shard_map/jit(cholesky)/cholesky | solution.py:19
  55.6 10.0 %custom-call.32 = f32[1,128,128]{1,2,0:T(8,128)S(1)} custom-call(f32[1,128,128]{2,1,0:T(8,128)S(1)} %get-tuple-element.62), custom_call_target="InvertDiagBlocksLowerTriangular" | custom-call | tf_op jit(solution)/shard_map/jit(cholesky)/cholesky | solution.py:19
  67.1 11.7 %cholesky.398 = f32[128,128]{1,0:T(8,128)S(1)} custom-call(f32[128,128]{1,0:T(8,128)S(1)} %cholesky.448), custom_call_target="Cholesky" | custom-call | tf_op jit(solution)/shard_map/jit(cholesky)/cholesky | solution.py:19
  79.6 9.8 %custom-call.33 = f32[1,128,128]{1,2,0:T(8,128)S(1)} custom-call(f32[1,128,128]{2,1,0:T(8,128)S(1)} %get-tuple-element.59), custom_call_target="InvertDiagBlocksLowerTriangular" | custom-call | tf_op jit(solution)/shard_map/jit(cholesky)/cholesky | solution.py:19
  90.8 12.1 %cholesky.415 = f32[128,128]{1,0:T(8,128)S(1)} custom-call(f32[128,128]{1,0:T(8,128)S(1)} %convolution_subtract_fusion.10), custom_call_target="Cholesky" | custom-call | tf_op jit(solution)/shard_map/jit(cholesky)/cholesky | solution.py:19
  107.9 11.7 %while.5 = (s32[]{:T(128)}, f32[512,512]{1,0:T(8,128)}, s32[4,2]{0,1:T(2,128)S(1)}, f32[4,128,128]{2,1,0:T(8,128)S(1)}, s32[]{:T(128)}) while((s32[]{:T(128)}, f32[512,512]{1,0:T(8,128)}, s32[4,2]{0,1:T(2,128)S(1)}, f32[4,128,128]{2,1,0:T(8,128)S(1)}, s32[]{:T(128)}) %tuple.61), condition=%wide.while_cond.clone, body=%wide.while_body.clone.sunk | while | flops 2 | bytes 131189 | solution.py:20
  108.6 2.2 bitcast_dynamic-update-slice_fusion.5
  111.5 2.2 bitcast_dynamic-update-slice_fusion.5
  114.5 2.2 bitcast_dynamic-update-slice_fusion.5
  117.4 2.2 bitcast_dynamic-update-slice_fusion.5
  119.6 39.3 %custom-call.34 = f32[4,128,128]{1,2,0:T(8,128)S(1)} custom-call(f32[4,128,128]{2,1,0:T(8,128)S(1)} %get-tuple-element.19), custom_call_target="InvertDiagBlocksLowerTriangular" | custom-call | tf_op jit(solution)/shard_map/jit(_solve_triangular)/triangular_solve | solution.py:20
  159.4 1.4 convolution_subtract_fusion.1
  161.3 1.9 convolution_subtract_fusion
  163.6 2.4 convolution_subtract_fusion.4
  166.4 2.9 fusion.8
  169.5 1.3 copy.8
  170.8 1.5 fusion.18
  172.3 11.7 %cholesky.286 = f32[128,128]{1,0:T(8,128)S(1)} custom-call(f32[128,128]{1,0:T(8,128)S(1)} %cholesky.426), custom_call_target="Cholesky" | custom-call | tf_op jit(solution)/shard_map/jit(cholesky)/cholesky | solution.py:19
  184.1 10.0 %custom-call.27 = f32[1,128,128]{1,2,0:T(8,128)S(1)} custom-call(f32[1,128,128]{2,1,0:T(8,128)S(1)} %get-tuple-element.55), custom_call_target="InvertDiagBlocksLowerTriangular" | custom-call | tf_op jit(solution)/shard_map/jit(cholesky)/cholesky | solution.py:19
  194.8 11.7 %cholesky.305 = f32[128,128]{1,0:T(8,128)S(1)} custom-call(f32[128,128]{1,0:T(8,128)S(1)} %cholesky.430), custom_call_target="Cholesky" | custom-call | tf_op jit(solution)/shard_map/jit(cholesky)/cholesky | solution.py:19
  206.6 9.8 %custom-call.28 = f32[1,128,128]{1,2,0:T(8,128)S(1)} custom-call(f32[1,128,128]{2,1,0:T(8,128)S(1)} %get-tuple-element.52), custom_call_target="InvertDiagBlocksLowerTriangular" | custom-call | tf_op jit(solution)/shard_map/jit(cholesky)/cholesky | solution.py:19
  217.1 11.7 %cholesky.326 = f32[128,128]{1,0:T(8,128)S(1)} custom-call(f32[128,128]{1,0:T(8,128)S(1)} %cholesky.435), custom_call_target="Cholesky" | custom-call | tf_op jit(solution)/shard_map/jit(cholesky)/cholesky | solution.py:19
  229.6 10.0 %custom-call.29 = f32[1,128,128]{1,2,0:T(8,128)S(1)} custom-call(f32[1,128,128]{2,1,0:T(8,128)S(1)} %get-tuple-element.49), custom_call_target="InvertDiagBlocksLowerTriangular" | custom-call | tf_op jit(solution)/shard_map/jit(cholesky)/cholesky | solution.py:19
  240.2 11.7 %cholesky.343 = f32[128,128]{1,0:T(8,128)S(1)} custom-call(f32[128,128]{1,0:T(8,128)S(1)} %convolution_subtract_fusion.11), custom_call_target="Cholesky" | custom-call | tf_op jit(solution)/shard_map/jit(cholesky)/cholesky | solution.py:19
  256.6 10.6 %while.4 = (s32[]{:T(128)}, f32[512,512]{1,0:T(8,128)S(1)}, s32[4,2]{0,1:T(2,128)S(1)}, f32[4,128,128]{2,1,0:T(8,128)}, s32[]{:T(128)}) while((s32[]{:T(128)}, f32[512,512]{1,0:T(8,128)S(1)}, s32[4,2]{0,1:T(2,128)S(1)}, f32[4,128,128]{2,1,0:T(8,128)}, s32[]{:T(128)}) %tuple.75), condition=%wide.while_cond, body=%wide.while_body.sunk | while | flops 2 | bytes 132205 | solution.py:20
  257.3 2.0 bitcast_dynamic-update-slice_fusion.4
  259.9 2.0 bitcast_dynamic-update-slice_fusion.4
  262.6 2.0 bitcast_dynamic-update-slice_fusion.4
  265.2 2.0 bitcast_dynamic-update-slice_fusion.4
  267.2 40.6 %custom-call.30 = f32[4,128,128]{1,2,0:T(8,128)S(1)} custom-call(f32[4,128,128]{2,1,0:T(8,128)} %get-tuple-element.18), custom_call_target="InvertDiagBlocksLowerTriangular" | custom-call | tf_op jit(solution)/shard_map/jit(_solve_triangular)/triangular_solve | solution.py:20
  310.7 1.5 convolution_subtract_fusion.5
  312.6 1.9 fusion
  317.7 55.8 %all-gather.2.cloned.1.call-done = bf16[4096,1024]{1,0:T(8,128)(2,1)} async-done(((bf16[256,1024]{1,0:T(8,128)(2,1)}), bf16[4096,1024]{1,0:T(8,128)(2,1)}) %all-gather.2.cloned.1.call-update) | async-done | bytes 8388624 | tf_op jit(solution)/shard_map/all_gather | solution.py:57
  373.5 5.4 dynamic-slice_select_fusion
  379.0 110.3 %all-reduce.4.cloned.1.call-done = bf16[2048,1024]{1,0:T(8,128)(2,1)} async-done(((bf16[2048,1024]{1,0:T(8,128)(2,1)}), bf16[2048,1024]{1,0:T(8,128)(2,1)}) %all-reduce.4.cloned.1.call-update) | async-done | bytes 4194320 | tf_op jit(solution)/shard_map/psum | solution.py:12
  489.3 23.8 %convolution_bitcast_fusion = f32[4096,1024]{0,1:T(8,128)} fusion(bf16[2048,1024]{1,0:T(8,128)(2,1)} %all-reduce.4.cloned.1.call-done, bf16[4096,2048]{1,0:T(8,128)(2,1)} %param.12), kind=kOutput, calls=%fused_computation.4 | convolution fusion | flops 17179869184 | bytes 37748736 | tf_op jit(solution)/shard_map/dot_general | solution.py:66
  513.1 95.7 %reduce-scatter.2.cloned.1.call-done = f32[256,1024]{0,1:T(8,128)} async-done(((f32[4096,1024]{0,1:T(8,128)}), f32[256,1024]{0,1:T(8,128)}) %reduce-scatter.2.cloned.1.call-update) | async-done | bytes 1048592 | tf_op jit(solution)/shard_map/reduce_scatter | solution.py:68
  608.9 1.7 convolution_bitcast_fusion.1
  610.6 1.8 convolution_bitcast_fusion.2
  612.5 1.5 pad_maximum_fusion
  615.2 150.4 %all-reduce.6.cloned.1.call-done = f32[2,512,512]{2,1,0:T(8,128)} async-done(((f32[2,512,512]{2,1,0:T(8,128)}), f32[2,512,512]{2,1,0:T(8,128)}) %all-reduce.6.cloned.1.call-update) | async-done | bytes 2097168 | tf_op jit(solution)/shard_map/psum | solution.py:85
  765.5 3.4 maximum_add_fusion
  (94 shorter events, 32.9 us)
Async XLA Ops:
  7.2 366.4 %all-gather.2.cloned.1.call-start = ((), (), s32[]{:S(2)}) async-start(), calls=%async_computation.1 | async-start | bytes 8912896 | tf_op jit(solution)/shard_map/all_gather | solution.py:57
  18.6 1.0 copy-start.2
  267.2 47.4 %copy-start.1 = (f32[512,512]{1,0:T(8,128)S(1)}, f32[512,512]{1,0:T(8,128)}, u32[]{:S(2)}) copy-start(f32[512,512]{1,0:T(8,128)} %fusion.8) | copy-start | bytes 3145732
  307.8 6.8 copy-start.3
  317.7 171.6 %all-reduce.4.cloned.1.call-start = ((), (), s32[]{:S(2)}) async-start(), calls=%async_computation.2 | async-start | bytes 8388608 | tf_op jit(solution)/shard_map/psum | solution.py:12
  378.9 229.9 %reduce-scatter.2.cloned.1.call-start = ((), (), s32[]{:S(2)}) async-start(), calls=%async_computation.3 | async-start | bytes 17825792 | tf_op jit(solution)/shard_map/reduce_scatter | solution.py:68
  513.1 252.5 %all-reduce.6.cloned.1.call-start = ((), (), s32[]{:S(2)}) async-start(), calls=%async_computation.4 | async-start | bytes 4194304 | tf_op jit(solution)/shard_map/psum | solution.py:85
  610.6 3.4 copy-start
Sparse Core Ops, SparseCore 0:
  317.8 55.7 all-gather.1
  379.1 110.1 all-reduce.3
  513.2 95.6 reduce-scatter.1
  614.1 151.3 all-reduce.5
where the time goes:
time: 785 us; the launch traced here: 776 us
  waiting for transfers between devices  412 us (52%)
  other arithmetic  256 us (33%)
  matrix products  53.9 us (7%)
  local copies, waits for them, and re-layouts  33.7 us (4%)
  between operations  19.5 us (2%)
    another operation x28, other arithmetic, factor_inverse(): factor_lower = jnp.linalg.cholesky(shifted)  158 us
    psum x1, waiting for transfers between devices, local(): totals = lax.psum(jnp.stack(diagonal_terms), ('row', 'col'))  150 us
    psum x1, waiting for transfers between devices, from_root(): return lax.psum(kept, axis)  110 us
    reduce_scatter x1, waiting for transfers between devices, local(): lax.psum_scatter(product(jnp.int32(0), own_rows * lax.axis_size('col')),...  95.7 us
    another operation x5, other arithmetic, factor_inverse(): jax.scipy.linalg.solve_triangular(factor_lower, identity, lower=True)  81.2 us
    all_gather x1, waiting for transfers between devices, local(): row_block = lax.all_gather(groups, 'col', axis=0, tiled=True)  55.8 us
    dot_general x1, matrix products, product(): jnp.dot(ancestor_inverse, column_block, preferred_element_type=jnp.float32)  23.8 us
    another operation x27, local copies, waits for them, and re-layouts, factor_inverse(): jax.scipy.linalg.solve_triangular(factor_lower, identity, lower=True)  22.9 us
  transfers between devices with their start and end apart: 4, of which 4 were waited for; matrix products, arithmetic and copies ran while one was open for 0% of the time, Pallas kernels for 0%

commit v1 on v0

--- a/solution.py
+++ b/solution.py
@@ -54,7 +54,9 @@
     own_rows = ancestor_inverse.shape[0] // lax.axis_size("col")
     panel_terms = []
     diagonal_terms = []
-    row_block = lax.all_gather(groups, "col", axis=0, tiled=True)
+    row_block = jnp.concatenate(
+        lax.all_to_all(jnp.stack([groups] * lax.axis_size("col")), "col", 0, 0), axis=0
+    )
     block_rows = row_block.shape[0] // col_ratio
     column_part = lax.dynamic_slice_in_dim(
         row_block, col_index % col_ratio * block_rows, block_rows, 0

time: 785 us -> 854 us (1.088)
  waiting for transfers between devices: 412 us -> 470 us
    all_to_all x0 -> x1, waiting for transfers between devices: none -> 112 us  [local(): lax.all_to_all(jnp.stack([groups] * lax.axis_size('col')), 'col', 0, 0)]
    all_gather x1 -> x0, waiting for transfers between devices: 55.8 us -> none  [local(): row_block = lax.all_gather(groups, 'col', axis=0, tiled=True)]
where the time goes in v1:
time: 854 us; the launch traced here: 844 us
  waiting for transfers between devices  470 us (55%)
  other arithmetic  255 us (30%)
  matrix products  53.9 us (6%)
  local copies, waits for them, and re-layouts  38 us (4%)
  between operations  19.5 us (2%)
    another operation x28, other arithmetic, factor_inverse(): factor_lower = jnp.linalg.cholesky(shifted)  158 us
    psum x1, waiting for transfers between devices, local(): totals = lax.psum(jnp.stack(diagonal_terms), ('row', 'col'))  151 us
    all_to_all x1, waiting for transfers between devices, local(): lax.all_to_all(jnp.stack([groups] * lax.axis_size('col')), 'col', 0, 0)  112 us
    psum x1, waiting for transfers between devices, from_root(): return lax.psum(kept, axis)  111 us
    reduce_scatter x1, waiting for transfers between devices, local(): lax.psum_scatter(product(jnp.int32(0), own_rows * lax.axis_size('col')),...  95.7 us
    another operation x5, other arithmetic, factor_inverse(): jax.scipy.linalg.solve_triangular(factor_lower, identity, lower=True)  81.2 us
    dot_general x1, matrix products, product(): jnp.dot(ancestor_inverse, column_block, preferred_element_type=jnp.float32)  23.8 us
    another operation x27, local copies, waits for them, and re-layouts, factor_inverse(): jax.scipy.linalg.solve_triangular(factor_lower, identity, lower=True)  22.9 us
  transfers between devices with their start and end apart: 4, of which 4 were waited for; matrix products, arithmetic and copies ran while one was open for 0% of the time, Pallas kernels for 0%

profile of v1, /device:TPU:1, one launch (start us, length us, event | category | flops | bytes accessed | tf_op | source)
XLA Modules:
  0.0 843.9 jit_solution(8605765310299673890)
XLA Ops:
  8.8 2.7 fusion.90
  11.8 1.6 copy.13
  14.5 2.5 copy.10
  17.1 1.5 fusion.17
  19.5 11.7 %cholesky.358 = f32[128,128]{1,0:T(8,128)S(1)} custom-call(f32[128,128]{1,0:T(8,128)S(1)} %cholesky.439), custom_call_target="Cholesky" | custom-call | tf_op jit(solution)/shard_map/jit(cholesky)/cholesky | solution.py:19
  31.3 9.8 %custom-call.31 = f32[1,128,128]{1,2,0:T(8,128)S(1)} custom-call(f32[1,128,128]{2,1,0:T(8,128)S(1)} %get-tuple-element.65), custom_call_target="InvertDiagBlocksLowerTriangular" | custom-call | tf_op jit(solution)/shard_map/jit(cholesky)/cholesky | solution.py:19
  43.8 11.7 %cholesky.377 = f32[128,128]{1,0:T(8,128)S(1)} custom-call(f32[128,128]{1,0:T(8,128)S(1)} %cholesky.443), custom_call_target="Cholesky" | custom-call | tf_op jit(solution)/shard_map/jit(cholesky)/cholesky | solution.py:19
  55.5 10.0 %custom-call.32 = f32[1,128,128]{1,2,0:T(8,128)S(1)} custom-call(f32[1,128,128]{2,1,0:T(8,128)S(1)} %get-tuple-element.62), custom_call_target="InvertDiagBlocksLowerTriangular" | custom-call | tf_op jit(solution)/shard_map/jit(cholesky)/cholesky | solution.py:19
  67.1 11.7 %cholesky.398 = f32[128,128]{1,0:T(8,128)S(1)} custom-call(f32[128,128]{1,0:T(8,128)S(1)} %cholesky.448), custom_call_target="Cholesky" | custom-call | tf_op jit(solution)/shard_map/jit(cholesky)/cholesky | solution.py:19
  79.5 9.8 %custom-call.33 = f32[1,128,128]{1,2,0:T(8,128)S(1)} custom-call(f32[1,128,128]{2,1,0:T(8,128)S(1)} %get-tuple-element.59), custom_call_target="InvertDiagBlocksLowerTriangular" | custom-call | tf_op jit(solution)/shard_map/jit(cholesky)/cholesky | solution.py:19
  90.8 12.1 %cholesky.415 = f32[128,128]{1,0:T(8,128)S(1)} custom-call(f32[128,128]{1,0:T(8,128)S(1)} %convolution_subtract_fusion.10), custom_call_target="Cholesky" | custom-call | tf_op jit(solution)/shard_map/jit(cholesky)/cholesky | solution.py:19
  107.8 11.7 %while.5 = (s32[]{:T(128)}, f32[512,512]{1,0:T(8,128)}, s32[4,2]{0,1:T(2,128)S(1)}, f32[4,128,128]{2,1,0:T(8,128)S(1)}, s32[]{:T(128)}) while((s32[]{:T(128)}, f32[512,512]{1,0:T(8,128)}, s32[4,2]{0,1:T(2,128)S(1)}, f32[4,128,128]{2,1,0:T(8,128)S(1)}, s32[]{:T(128)}) %tuple.61), condition=%wide.while_cond.clone, body=%wide.while_body.clone.sunk | while | flops 2 | bytes 131189 | solution.py:20
  108.5 2.2 bitcast_dynamic-update-slice_fusion.5
  111.5 2.2 bitcast_dynamic-update-slice_fusion.5
  114.4 2.2 bitcast_dynamic-update-slice_fusion.5
  117.3 2.2 bitcast_dynamic-update-slice_fusion.5
  119.5 39.3 %custom-call.34 = f32[4,128,128]{1,2,0:T(8,128)S(1)} custom-call(f32[4,128,128]{2,1,0:T(8,128)S(1)} %get-tuple-element.19), custom_call_target="InvertDiagBlocksLowerTriangular" | custom-call | tf_op jit(solution)/shard_map/jit(_solve_triangular)/triangular_solve | solution.py:20
  161.2 1.9 convolution_subtract_fusion
  163.5 2.4 convolution_subtract_fusion.4
  166.4 2.9 fusion.8
  170.8 1.5 fusion.18
  172.3 11.7 %cholesky.286 = f32[128,128]{1,0:T(8,128)S(1)} custom-call(f32[128,128]{1,0:T(8,128)S(1)} %cholesky.426), custom_call_target="Cholesky" | custom-call | tf_op jit(solution)/shard_map/jit(cholesky)/cholesky | solution.py:19
  184.0 10.0 %custom-call.27 = f32[1,128,128]{1,2,0:T(8,128)S(1)} custom-call(f32[1,128,128]{2,1,0:T(8,128)S(1)} %get-tuple-element.55), custom_call_target="InvertDiagBlocksLowerTriangular" | custom-call | tf_op jit(solution)/shard_map/jit(cholesky)/cholesky | solution.py:19
  194.8 11.7 %cholesky.305 = f32[128,128]{1,0:T(8,128)S(1)} custom-call(f32[128,128]{1,0:T(8,128)S(1)} %cholesky.430), custom_call_target="Cholesky" | custom-call | tf_op jit(solution)/shard_map/jit(cholesky)/cholesky | solution.py:19
  206.5 9.8 %custom-call.28 = f32[1,128,128]{1,2,0:T(8,128)S(1)} custom-call(f32[1,128,128]{2,1,0:T(8,128)S(1)} %get-tuple-element.52), custom_call_target="InvertDiagBlocksLowerTriangular" | custom-call | tf_op jit(solution)/shard_map/jit(cholesky)/cholesky | solution.py:19
  217.0 11.7 %cholesky.326 = f32[128,128]{1,0:T(8,128)S(1)} custom-call(f32[128,128]{1,0:T(8,128)S(1)} %cholesky.435), custom_call_target="Cholesky" | custom-call | tf_op jit(solution)/shard_map/jit(cholesky)/cholesky | solution.py:19
  229.5 10.0 %custom-call.29 = f32[1,128,128]{1,2,0:T(8,128)S(1)} custom-call(f32[1,128,128]{2,1,0:T(8,128)S(1)} %get-tuple-element.49), custom_call_target="InvertDiagBlocksLowerTriangular" | custom-call | tf_op jit(solution)/shard_map/jit(cholesky)/cholesky | solution.py:19
  240.1 11.7 %cholesky.343 = f32[128,128]{1,0:T(8,128)S(1)} custom-call(f32[128,128]{1,0:T(8,128)S(1)} %convolution_subtract_fusion.11), custom_call_target="Cholesky" | custom-call | tf_op jit(solution)/shard_map/jit(cholesky)/cholesky | solution.py:19
  256.5 10.6 %while.4 = (s32[]{:T(128)}, f32[512,512]{1,0:T(8,128)S(1)}, s32[4,2]{0,1:T(2,128)S(1)}, f32[4,128,128]{2,1,0:T(8,128)}, s32[]{:T(128)}) while((s32[]{:T(128)}, f32[512,512]{1,0:T(8,128)S(1)}, s32[4,2]{0,1:T(2,128)S(1)}, f32[4,128,128]{2,1,0:T(8,128)}, s32[]{:T(128)}) %tuple.73), condition=%wide.while_cond, body=%wide.while_body.sunk | while | flops 2 | bytes 132205 | solution.py:20
  257.2 2.0 bitcast_dynamic-update-slice_fusion.4
  259.8 2.0 bitcast_dynamic-update-slice_fusion.4
  262.5 2.0 bitcast_dynamic-update-slice_fusion.4
  265.1 2.0 bitcast_dynamic-update-slice_fusion.4
  267.1 40.6 %custom-call.30 = f32[4,128,128]{1,2,0:T(8,128)S(1)} custom-call(f32[4,128,128]{2,1,0:T(8,128)} %get-tuple-element.18), custom_call_target="InvertDiagBlocksLowerTriangular" | custom-call | tf_op jit(solution)/shard_map/jit(_solve_triangular)/triangular_solve | solution.py:20
  310.6 1.5 convolution_subtract_fusion.5
  312.6 1.9 fusion
  316.8 4.3 stack.20
  321.1 7.3 all-to-all-start
  328.5 112.4 %all-to-all-done = bf16[16,256,1024]{2,1,0:T(8,128)(2,1)} async-done(((bf16[16,256,1024]{2,1,0:T(8,128)(2,1)}), bf16[16,256,1024]{2,1,0:T(8,128)(2,1)}, u32[]{:S(2)}, u32[]{:S(2)}) %all-to-all-start) | async-done | bytes 8388640 | tf_op jit(solution)/shard_map/all_to_all | solution.py:58
  440.9 5.4 dynamic-slice_select_fusion
  446.3 111.1 %all-reduce.4.cloned.1.call-done = bf16[2048,1024]{1,0:T(8,128)(2,1)} async-done(((bf16[2048,1024]{1,0:T(8,128)(2,1)}), bf16[2048,1024]{1,0:T(8,128)(2,1)}) %all-reduce.4.cloned.1.call-update) | async-done | bytes 4194320 | tf_op jit(solution)/shard_map/psum | solution.py:12
  557.4 23.8 %convolution_bitcast_fusion = f32[4096,1024]{0,1:T(8,128)} fusion(bf16[2048,1024]{1,0:T(8,128)(2,1)} %all-reduce.4.cloned.1.call-done, bf16[4096,2048]{1,0:T(8,128)(2,1)} %param.12), kind=kOutput, calls=%fused_computation.4 | convolution fusion | flops 17179869184 | bytes 37748736 | tf_op jit(solution)/shard_map/dot_general | solution.py:68
  581.3 95.7 %reduce-scatter.2.cloned.1.call-done = f32[256,1024]{0,1:T(8,128)} async-done(((f32[4096,1024]{0,1:T(8,128)}), f32[256,1024]{0,1:T(8,128)}) %reduce-scatter.2.cloned.1.call-update) | async-done | bytes 1048592 | tf_op jit(solution)/shard_map/reduce_scatter | solution.py:70
  677.0 1.7 convolution_bitcast_fusion.1
  678.8 1.8 convolution_bitcast_fusion.2
  680.6 1.5 pad_maximum_fusion
  683.3 150.5 %all-reduce.6.cloned.1.call-done = f32[2,512,512]{2,1,0:T(8,128)} async-done(((f32[2,512,512]{2,1,0:T(8,128)}), f32[2,512,512]{2,1,0:T(8,128)}) %all-reduce.6.cloned.1.call-update) | async-done | bytes 2097168 | tf_op jit(solution)/shard_map/psum | solution.py:87
  833.8 3.4 maximum_add_fusion
  (94 shorter events, 34.8 us)
Async XLA Ops:
  18.6 1.0 copy-start.2
  267.1 47.4 %copy-start.1 = (f32[512,512]{1,0:T(8,128)S(1)}, f32[512,512]{1,0:T(8,128)}, u32[]{:S(2)}) copy-start(f32[512,512]{1,0:T(8,128)} %fusion.8) | copy-start | bytes 3145732
  307.7 6.8 copy-start.3
  321.1 119.8 %all-to-all-start = ((bf16[16,256,1024]{2,1,0:T(8,128)(2,1)}), bf16[16,256,1024]{2,1,0:T(8,128)(2,1)}, u32[]{:S(2)}, u32[]{:S(2)}) async-start(bf16[16,256,1024]{2,1,0:T(8,128)(2,1)} %stack.20), calls=%async_computation | async-start | bytes 16777216 | tf_op jit(solution)/shard_map/all_to_all | solution.py:58
  328.4 229.0 %all-reduce.4.cloned.1.call-start = ((), (), s32[]{:S(2)}) async-start(), calls=%async_computation.2 | async-start | bytes 8388608 | tf_op jit(solution)/shard_map/psum | solution.py:12
  446.3 230.7 %reduce-scatter.2.cloned.1.call-start = ((), (), s32[]{:S(2)}) async-start(), calls=%async_computation.3 | async-start | bytes 17825792 | tf_op jit(solution)/shard_map/reduce_scatter | solution.py:70
  581.2 252.6 %all-reduce.6.cloned.1.call-start = ((), (), s32[]{:S(2)}) async-start(), calls=%async_computation.4 | async-start | bytes 4194304 | tf_op jit(solution)/shard_map/psum | solution.py:87
  678.7 3.4 copy-start
Sparse Core Ops, SparseCore 0:
  446.4 110.9 all-reduce.3
  581.3 95.6 reduce-scatter.1
  682.4 151.3 all-reduce.5
